TPU v7x, 512 devices: a whole 4x8x8 slice. The times are simulated.
512 devices in a mesh: seq: 64 (over z, x, core), head: 8 (over y).
Axes of the slice: x: 4, y: 8, z: 8, core: 2. Of those that a mesh axis runs over, the one named last changes fastest.
Arguments:
- query_rows: bfloat16 [32768, 64, 128], P('seq', 'head'), may hold values from -6 to 6
- key_rows: bfloat16 [32768, 64, 128], P('seq', 'head'), may hold values from -6 to 6
- value_rows: bfloat16 [32768, 64, 128], P('seq', 'head'), may hold values from -6 to 6
- log_decay: float32 [32768, 64], P('seq', 'head'), may hold values from -1.5 to 0, as said below
- state_in: float32 [128, 64, 128], P(None, 'head'), may hold values from -768 to 768
- decode_query: bfloat16 [8, 64, 128], P(None, 'head'), may hold values from -6 to 6
- decode_key: bfloat16 [8, 64, 128], P(None, 'head'), may hold values from -6 to 6
- decode_value: bfloat16 [8, 64, 128], P(None, 'head'), may hold values from -6 to 6
- decode_decay: float32 [8, 64], P(None, 'head'), may hold values from -0.5 to -0.02
Outputs:
- attended: bfloat16 [32768, 64, 128], P('seq', 'head')
- final_state: float32 [128, 64, 128], P('seq', 'head')
- decode_out: float32 [8, 64, 128], P(None, 'head')
Inputs may be any that keep to these rules, and one draw needn't show every extreme that they name: log_decay is never positive.
All inputs are finite; a program needn't handle non-finite values.
Results may differ from a plain program's by a relative error of at most 0.0035.
Values sent between devices are 32-bit elements; how exact they have to be, the bound alone decides.
A program may use at most 64 MiB of HBM per device.

v0:
```python
import functools

import jax
import jax.numpy as jnp
from jax import lax
from jax.sharding import Mesh
from jax.sharding import PartitionSpec as P

GROUP = 512
DECODE = 8
SEQ = ("seq_0", "seq_1", "seq_2")


norm_eps = 1e-06


def sent_to_all(array, axis):
    copies = jnp.broadcast_to(array, (lax.axis_size(axis), *array.shape))
    return lax.all_to_all(copies, axis, split_axis=0, concat_axis=0, tiled=True)


def joined_along(parts, dim):
    parts = jnp.moveaxis(parts, 0, dim)
    dims = parts.shape
    return parts.reshape(*dims[:dim], dims[dim] * dims[dim + 1], *dims[dim + 2 :])


def gathered_copies(array, axis, dim):
    parts = sent_to_all(array, axis)
    return joined_along(parts, dim)


def one_axis_at_a_time(array, axes):
    return functools.reduce(lax.psum, axes, array)


def normalize(mixed):
    return mixed * lax.rsqrt(jnp.mean(mixed * mixed, axis=-1, keepdims=True) + norm_eps)


def prefix_weights(decays):
    inclusive = jnp.cumsum(decays, axis=0)
    exclusive = inclusive - decays
    extent = decays.shape[0]
    order = jnp.arange(extent)
    earlier_mask = order[:, None] > order[None, :]
    gaps = exclusive[:, None, :] - inclusive[None, :, :]
    pair_weights = jnp.exp(jnp.where(earlier_mask[:, :, None], gaps, -jnp.inf))
    to_end = jnp.exp(inclusive[-1][None, :] - inclusive)
    return (pair_weights, to_end, exclusive, inclusive[-1])


def local(
    query_rows,
    key_rows,
    value_rows,
    log_decay,
    state_in,
    decode_query,
    decode_key,
    decode_value,
    decode_decay,
):
    tokens_here = query_rows.shape[0]
    heads_here = query_rows.shape[1]
    width = query_rows.shape[2]
    blocks = tokens_here // GROUP
    queries = query_rows.reshape(blocks, GROUP, heads_here, width)
    keys_blk = key_rows.reshape(blocks, GROUP, heads_here, width)
    values_blk = value_rows.reshape(blocks, GROUP, heads_here, width)
    cumulative = jnp.cumsum(log_decay.reshape(blocks, GROUP, heads_here), axis=1)
    transposed = jnp.transpose(cumulative, (0, 2, 1))
    token_positions = jnp.arange(GROUP)
    causal_mask = token_positions[:, None] >= token_positions[None, :]
    gaps = transposed[:, :, :, None] - transposed[:, :, None, :]
    factors = jnp.exp(jnp.where(causal_mask[None, None], gaps, -jnp.inf))
    scores = jnp.einsum("nihd,njhd->nhij", queries, keys_blk, preferred_element_type=jnp.float32)
    masked = (scores * factors).astype(jnp.bfloat16)
    intra = jnp.einsum("nhij,njhd->nihd", masked, values_blk, preferred_element_type=jnp.float32)
    block_last = cumulative[:, -1, :]
    weighted = (
        key_rows.reshape(blocks, GROUP, heads_here, width).astype(jnp.float32)
        * jnp.exp(block_last[:, None, :] - cumulative)[:, :, :, None]
    )
    value_wide = values_blk.astype(jnp.float32)
    block_states = jnp.einsum(
        "njhd,njhe->ndhe", weighted, value_wide, precision=lax.Precision.HIGHEST
    )
    block_pairs, block_to_end, block_before, shard_total = prefix_weights(block_last)
    local_prefix = jnp.einsum(
        "cfh,fdhe->cdhe", block_pairs, block_states, precision=lax.Precision.HIGHEST
    )
    shard_state = jnp.einsum(
        "fh,fdhe->dhe", block_to_end, block_states, precision=lax.Precision.HIGHEST
    )
    gathered = gathered_copies(shard_total[None, :], SEQ, 0)
    my_index = lax.axis_index(SEQ)
    shard_pairs, shard_to_end, shard_before, grand_total = prefix_weights(gathered)
    before_me = lax.dynamic_index_in_dim(shard_before, my_index, 0, keepdims=False)
    row_count = width // lax.axis_size(SEQ)
    row_start = my_index * row_count
    received = lax.all_to_all(shard_state[None], SEQ, split_axis=1, concat_axis=0, tiled=True)
    prefixes = jnp.einsum("efh,frhd->erhd", shard_pairs, received, precision=lax.Precision.HIGHEST)
    final_rows = jnp.einsum("fh,frhd->rhd", shard_to_end, received, precision=lax.Precision.HIGHEST)
    returned = lax.all_to_all(prefixes, SEQ, split_axis=0, concat_axis=1, tiled=True)
    carried = returned[0]
    prior_rows = lax.dynamic_slice_in_dim(state_in, row_start, row_count, 0)
    final_rows = final_rows + jnp.exp(grand_total)[None, :, None] * prior_rows
    incoming = jnp.exp(before_me)[None, :, None] * state_in + carried
    block_incoming = jnp.exp(block_before)[:, None, :, None] * incoming[None] + local_prefix
    inter = jnp.exp(cumulative)[:, :, :, None] * jnp.einsum(
        "nihd,ndhe->nihe",
        queries.astype(jnp.float32),
        block_incoming,
        precision=lax.Precision.HIGHEST,
    )
    attended = normalize(intra + inter).astype(jnp.bfloat16).reshape(tokens_here, heads_here, width)
    key_part = lax.dynamic_slice_in_dim(decode_key, row_start, row_count, 2).astype(jnp.float32)
    query_part = lax.dynamic_slice_in_dim(decode_query, row_start, row_count, 2).astype(jnp.float32)
    running = final_rows
    partials = []
    for step in range(DECODE):
        value_now = decode_value[step].astype(jnp.float32)
        running = (
            jnp.exp(decode_decay[step])[None, :, None] * running
            + key_part[step].T[:, :, None] * value_now[None, :, :]
        )
        partials.append(
            jnp.einsum("hr,rhe->he", query_part[step], running, precision=lax.Precision.HIGHEST)
        )
    readings = one_axis_at_a_time(jnp.stack(partials, axis=0), SEQ)
    decode_out = normalize(readings)
    return (attended, final_rows, decode_out)


def solution(mesh):
    split = Mesh(
        mesh.devices.reshape(8, 4, 2, mesh.shape["head"]), ("seq_0", "seq_1", "seq_2", "head")
    )
    return jax.shard_map(
        local,
        mesh=split,
        in_specs=(
            P(SEQ, "head", None),
            P(SEQ, "head", None),
            P(SEQ, "head", None),
            P(SEQ, "head"),
            P(None, "head", None),
            P(None, "head", None),
            P(None, "head", None),
            P(None, "head", None),
            P(None, "head"),
        ),
        out_specs=(P(SEQ, "head", None), P(SEQ, "head", None), P(None, "head", None)),
        check_vma=False,
    )
```

profile of v0, /device:TPU:1, one launch (start us, length us, event | category | flops | bytes accessed | tf_op | source)
XLA Modules:
  0.0 133.6 jit_solution(16621897648863228565)
XLA Ops:
  0.6 2.3 %reduce-window.6 = f32[1,8,4,128]{3,1,2,0:T(8,128)S(1)} reduce-window(f32[1,8,4,128]{3,1,2,0:T(8,128)} %bitcast.231, f32[]{:T(128)} %constant.20.clone.1), window={size=1x1x1x128 pad=0_0x0_0x0_0x127_0}, to_apply=%region_0.0 | reduce-window | flops 520192 | bytes 32772 | tf_op jit(solution)/shard_map/reduce-window
  2.9 0.2 slice_reduce_fusion
  3.2 0.2 slice_reduce_fusion.1
  3.4 0.6 broadcast_in_dim.38
  4.1 14.8 %all-to-all-start = ((f32[64,1,8]{2,1,0:T(1,128)}), f32[64,1,8]{2,1,0:T(1,128)S(1)}, u32[]{:S(2)}, u32[]{:S(2)}) async-start(f32[64,1,8]{2,1,0:T(1,128)} %broadcast_in_dim.38), calls=%async_computation | async-start | bytes 65536 | tf_op jit(solution)/shard_map/all_to_all | solution.py:19
  19.0 0.1 iota_compare_fusion
  19.1 0.1 copy.135
  19.3 0.8 dynamic-slice_convert_fusion
  20.1 0.8 bitcast_convert_fusion.7
  20.9 1.8 %convert_multiply_fusion = f32[512,8,128]{2,1,0:T(8,128)S(1)} fusion(bf16[512,8,128]{2,1,0:T(8,128)(2,1)} %param.10, f32[512,8]{1,0:T(8,128)S(1)} %copy.135), kind=kLoop, calls=%fused_computation.13 | loop fusion | flops 1048576 | bytes 3162112 | tf_op jit(solution)/shard_map/mul | solution.py:82
  22.7 2.0 %fusion.8 = f32[8,128,128]{2,1,0:T(8,128)S(1)} fusion(f32[512,8,128]{2,1,0:T(8,128)S(1)} %convert_multiply_fusion, bf16[512,8,128]{2,1,0:T(8,128)(2,1)S(1)} %copy-done), kind=kOutput, calls=%fused_computation.9 | convolution fusion | flops 805306368 | bytes 3670016 | tf_op jit(solution)/shard_map/njhd,njhe->ndhe/dot_general | solution.py:86
  24.7 0.1 multiply_bitcast_fusion
  24.9 6.1 %fusion = f32[8,512,128]{1,2,0:T(8,128)} fusion(f32[8,512]{1,0:T(8,128)S(1)} %bitcast_add_fusion.2, pred[512,512]{1,0:T(8,128)(4,1)S(1)} %iota_compare_fusion, bf16[512,8,128]{2,1,0:T(8,128)(2,1)S(1)} %copy-done.1, bf16[512,8,128]{2,1,0:T(8,128)(2,1)S(1)} %copy-done, bf16[512,8,128]{2,1,0:T(8,128)(2,1)} %param.9), kind=kOutput, calls=%fused_computation.1 | convolution fusion | flops 1082130432 | bytes 5521408 | tf_op jit(solution)/shard_map/nhij,njhd->nihd/dot_general | solution.py:79
  31.0 1.1 copy.138
  32.1 10.3 %all-to-all-start.1 = ((f32[1,128,8,128]{3,2,0,1:T(8,128)}), f32[1,128,8,128]{3,2,0,1:T(8,128)S(1)}, u32[]{:S(2)}, u32[]{:S(2)}) async-start(f32[1,128,8,128]{3,2,0,1:T(8,128)} %copy.138), calls=%async_computation.1 | async-start | bytes 1048576 | tf_op jit(solution)/shard_map/all_to_all | solution.py:102
  42.5 0.1 constant_dynamic-slice_fusion.8
  42.6 0.1 copy.162
  42.6 0.1 copy.148
  42.7 0.1 copy.150
  42.8 0.1 copy.152
  42.9 0.1 copy.154
  43.0 0.1 copy.156
  43.0 0.1 copy.158
  43.1 0.1 copy.160
  43.2 0.1 copy.147
  43.3 0.1 copy.168
  43.4 0.1 copy.149
  43.5 0.1 copy.171
  43.6 0.1 copy.151
  43.7 0.1 copy.174
  43.8 0.1 copy.153
  43.9 0.1 copy.177
  44.0 0.1 copy.155
  44.1 0.1 copy.180
  44.2 0.1 copy.157
  44.3 0.1 copy.183
  44.4 0.1 copy.159
  44.5 0.1 copy.186
  44.6 0.1 copy.161
  44.7 0.1 copy.189
  44.8 0.1 reduce_window_sum.51
  45.1 15.0 %all-to-all-done.1 = f32[1,128,8,128]{3,2,0,1:T(8,128)S(1)} async-done(((f32[1,128,8,128]{3,2,0,1:T(8,128)}), f32[1,128,8,128]{3,2,0,1:T(8,128)S(1)}, u32[]{:S(2)}, u32[]{:S(2)}) %all-to-all-start.1) | async-done | bytes 524320 | tf_op jit(solution)/shard_map/all_to_all | solution.py:102
  60.1 0.5 fusion.25
  60.7 1.4 %multiply_add_fusion = (f32[2,8,128]{2,1,0:T(8,128)S(1)}, f32[2,8,128]{2,1,0:T(8,128)S(1)}, f32[2,8,128]{2,1,0:T(8,128)S(1)}, f32[2,8,128]{2,1,0:T(8,128)S(1)}, ...) fusion(f32[8,128]{1,0:T(8,128)S(1)} %get-tuple-element.53, ...), kind=kLoop, calls=%fused_computation.67 | loop fusion | flops 53248 | bytes 123684 | tf_op jit(solution)/shard_map/add | solution.py:125
  62.1 0.2 fusion.55
  62.2 0.7 convolution_bitcast_fusion
  63.0 1.2 copy.143
  64.2 5.7 %all-to-all-start.2 = ((f32[64,2,8,128]{3,1,2,0:T(2,128)}), f32[64,2,8,128]{3,1,2,0:T(2,128)S(1)}, u32[]{:S(2)}, u32[]{:S(2)}) async-start(f32[64,2,8,128]{3,1,2,0:T(2,128)} %copy.143), calls=%async_computation.2 | async-start | bytes 1048576 | tf_op jit(solution)/shard_map/all_to_all | solution.py:105
  69.9 0.1 fusion.53
  70.1 0.2 fusion.51
  70.2 0.2 fusion.49
  70.4 0.2 fusion.47
  70.6 0.2 fusion.45
  70.7 0.2 fusion.43
  70.9 0.2 fusion.41
  71.1 29.5 %psum.21 = f32[8,8,128]{2,1,0:T(8,128)S(1)} all-reduce(f32[8,8,128]{2,1,0:T(8,128)S(1)} %constant_dynamic-update-slice_fusion), channel_id=1, replica_groups=mesh['seq_0'=8,'seq_1'=4,'seq_2'=2,'head'=8] {'seq_0'}, use_global_device_ids=true, to_apply=%region_4.5 | all-reduce | flops 8192 | bytes 65536 | tf_op jit(solution)/shard_map/psum | solution.py:34
  100.5 13.2 %psum.22 = f32[8,8,128]{2,1,0:T(8,128)S(1)} all-reduce(f32[8,8,128]{2,1,0:T(8,128)S(1)} %psum.21), channel_id=1, replica_groups=mesh['seq_0'=8,'seq_1'=4,'seq_2'=2,'head'=8] {'seq_1'}, use_global_device_ids=true, to_apply=%region_5.6 | all-reduce | flops 8192 | bytes 65536 | tf_op jit(solution)/shard_map/psum | solution.py:34
  113.8 13.8 %psum.23 = f32[8,8,128]{2,1,0:T(8,128)S(1)} all-reduce(f32[8,8,128]{2,1,0:T(8,128)S(1)} %psum.22), channel_id=1, replica_groups=mesh['seq_0'=8,'seq_1'=4,'seq_2'=2,'head'=8] {'seq_2'}, use_global_device_ids=true, to_apply=%region_6.7 | all-reduce | flops 8192 | bytes 65536 | tf_op jit(solution)/shard_map/psum | solution.py:34
  127.6 0.1 multiply_reduce_fusion.1
  127.7 0.7 broadcast_multiply_fusion
  128.4 0.2 copy.144
  128.6 3.2 %multiply_reduce_fusion = (f32[512,8]{0,1:T(8,128)S(1)}, f32[1,512,8,128]{1,3,2,0:T(8,128)S(1)}) fusion(bf16[512,8,128]{2,1,0:T(8,128)(2,1)S(1)} %copy-done.2, f32[128,8,128]{2,0,1:T(8,128)S(1)} %bitcast.227, f32[128,8,128]{2,1,0:T(8,128)} %param.13, f32[8,128,128]{2,1,0:T(8,128)S(1)} %fusion.8, f32[8]{0:T(128)S(1)} %get-tuple-element.30, ...), kind=kOutput, calls=%fused_computation.12 | convolution fusion | flops 808054784 | bytes 6848576 | tf_op jit(solution)/shard_map/nihd,ndhe->nihe/dot_general | solution.py:111
  131.9 0.3 fusion.10
  132.2 1.5 %copy.163 = bf16[512,8,128]{2,1,0:T(8,128)(2,1)} copy(bf16[512,8,128]{0,2,1:T(8,128)(2,1)S(1)} %fusion.10) | data formatting | bytes 2097152
  (38 shorter events, 0.6 us)
Async XLA Ops:
  0.6 22.1 %copy-start = (bf16[512,8,128]{2,1,0:T(8,128)(2,1)S(1)}, bf16[512,8,128]{2,1,0:T(8,128)(2,1)}, u32[]{:S(2)}) copy-start(bf16[512,8,128]{2,1,0:T(8,128)(2,1)} %param.11) | copy-start | bytes 3145732
  4.1 28.1 %all-to-all-start = ((f32[64,1,8]{2,1,0:T(1,128)}), f32[64,1,8]{2,1,0:T(1,128)S(1)}, u32[]{:S(2)}, u32[]{:S(2)}) async-start(f32[64,1,8]{2,1,0:T(1,128)} %broadcast_in_dim.38), calls=%async_computation | async-start | bytes 65536 | tf_op jit(solution)/shard_map/all_to_all | solution.py:19
  22.7 2.1 %copy-start.1 = (bf16[512,8,128]{2,1,0:T(8,128)(2,1)S(1)}, bf16[512,8,128]{2,1,0:T(8,128)(2,1)}, u32[]{:S(2)}) copy-start(bf16[512,8,128]{2,1,0:T(8,128)(2,1)} %param.10) | copy-start | bytes 3145732
  24.8 6.2 %copy-start.4 = (f32[8,8]{1,0:T(8,128)S(1)}, f32[8,8]{1,0:T(8,128)}, u32[]{:S(2)}) copy-start(f32[8,8]{1,0:T(8,128)} %param.17) | copy-start | bytes 772
  31.0 11.4 %copy-start.3 = (bf16[8,8,128]{2,1,0:T(8,128)(2,1)S(1)}, bf16[8,8,128]{2,1,0:T(8,128)(2,1)}, u32[]{:S(2)}) copy-start(bf16[8,8,128]{2,1,0:T(8,128)(2,1)} %param.14) | copy-start | bytes 49156
  32.1 28.0 %all-to-all-start.1 = ((f32[1,128,8,128]{3,2,0,1:T(8,128)}), f32[1,128,8,128]{3,2,0,1:T(8,128)S(1)}, u32[]{:S(2)}, u32[]{:S(2)}) async-start(f32[1,128,8,128]{3,2,0,1:T(8,128)} %copy.138), calls=%async_computation.1 | async-start | bytes 1048576 | tf_op jit(solution)/shard_map/all_to_all | solution.py:102
  63.0 65.6 %copy-start.2 = (bf16[512,8,128]{2,1,0:T(8,128)(2,1)S(1)}, bf16[512,8,128]{2,1,0:T(8,128)(2,1)}, u32[]{:S(2)}) copy-start(bf16[512,8,128]{2,1,0:T(8,128)(2,1)} %param.9) | copy-start | bytes 3145732
  64.2 64.2 %all-to-all-start.2 = ((f32[64,2,8,128]{3,1,2,0:T(2,128)}), f32[64,2,8,128]{3,1,2,0:T(2,128)S(1)}, u32[]{:S(2)}, u32[]{:S(2)}) async-start(f32[64,2,8,128]{3,1,2,0:T(2,128)} %copy.143), calls=%async_computation.2 | async-start | bytes 1048576 | tf_op jit(solution)/shard_map/all_to_all | solution.py:105
where the time goes:
time: 134 us
  blocking collectives  56.5 us (42%)
  starting transfers between devices  30.8 us (23%)
  waiting for transfers between devices  15 us (11%)
  matrix products  13.8 us (10%)
  other arithmetic  8.84 us (7%)
  local copies, waits for them, and re-layouts  7.65 us (6%)
    psum x3, blocking collectives, one_axis_at_a_time(): return functools.reduce(lax.psum, axes, array)  56.5 us
    all_to_all x1, waiting for transfers between devices, local(): lax.all_to_all(shard_state[None], SEQ, split_axis=1, concat_axis=0, tiled...  15 us
    all_to_all x1, starting transfers between devices, sent_to_all(): return lax.all_to_all(copies, axis, split_axis=0, concat_axis=0, tiled=True)  14.8 us
    all_to_all x1, starting transfers between devices, local(): lax.all_to_all(shard_state[None], SEQ, split_axis=1, concat_axis=0, tiled...  10.3 us
    dot_general x1, matrix products, local(): jnp.einsum('nhij,njhd->nihd', masked, values_blk, preferred_element_type=...  6.14 us
    all_to_all x1, starting transfers between devices, local(): lax.all_to_all(prefixes, SEQ, split_axis=0, concat_axis=1, tiled=True)  5.69 us
    dot_general x1, matrix products, local(): jnp.einsum('nihd,ndhe->nihe', queries.astype(jnp.float32), block_incoming...  3.24 us
  transfers between devices with their start and end apart: 3, of which 1 were waited for; matrix products, arithmetic and copies ran while one was open for 13% of the time, Pallas kernels for 0%

commit v1 on v0

v1 whole, which is shorter than its diff:
```python
import functools

import jax
import jax.numpy as jnp
from jax import lax
from jax.experimental import pallas as pl
from jax.experimental.pallas import tpu as pltpu
from jax.sharding import Mesh
from jax.sharding import PartitionSpec as P

GROUP = 512
DECODE = 8
DH = 128
HEADS = 8
X, C = 4, 2
SEQ = ("seq_0", "seq_1", "seq_2")
MESH = pl.DeviceIdType.MESH
F32, BF16 = jnp.float32, jnp.bfloat16
norm_eps = 1e-06

HALF = 256
QUARTER = 64
DECAY = HALF
EXTRA = HALF + 8
CORE_ROWS = HALF + 8 + 32
X_ROWS = QUARTER + 16

FILL = ((0, 2), (2, 5), (5, 8))


def halves(wide):
    high = wide.astype(BF16)
    return high, (wide - high.astype(F32)).astype(BF16)


def dot(a, b):
    return jnp.dot(a, b, preferred_element_type=F32)


def dot_nt(a, b):
    return lax.dot_general(a, b, (((1,), (1,)), ((), ())), preferred_element_type=F32)


def scaled(tile, rows):
    count = rows.shape[0]
    return (rows.reshape(count // 8, 8, DH) * tile[None]).reshape(count, DH)


def kernel(
    Z,
    q_hbm, k_hbm, v_hbm, ld_hbm, si_hbm, dq_hbm, dk_hbm, dv_hbm, dd_hbm,
    out_hbm, fs_ref, dec_ref,
    kb, vb, qb, kf, vf, qf, ldb, si, dqb, dkb, dvb, ddb, dqf, dkf, dvf,
    perm_s, cum_s, w_s, kT, vh, qp, ecol, intra, ob,
    bbuf, cbuf, tbuf, xbuf, rbuf, zbuf, zs, zr, xs, pc, ps, pp,
    sitile, rin, dint, dexp,
    in_sem, out_sem,
    core_s, core_r, x_s, x_r, z_s, z_r, zr_s, zr_r, xr_s, xr_r, cr_s, cr_r,
):
    ZR = QUARTER // Z
    R = ZR // 4
    zi, xi, ci = (lax.axis_index(a) for a in SEQ)
    first = ci == 0

    half = GROUP // 2
    copies = {}

    def fetch(name, src, dst, slot):
        copies[name] = pltpu.make_async_copy(src, dst, in_sem.at[slot])
        copies[name].start()

    fetch("ld", ld_hbm, ldb, 0)
    for i in range(2):
        rows = pl.ds(i * half, half)
        fetch(f"k{i}", k_hbm.at[rows], kb.at[rows], 1 + i)
    for i in range(2):
        rows = pl.ds(i * half, half)
        fetch(f"v{i}", v_hbm.at[rows], vb.at[rows], 3 + i)
    fetch("dq", dq_hbm, dqb, 5)
    fetch("q", q_hbm, qb, 6)
    fetch("dk", dk_hbm, dkb, 7)
    fetch("dv", dv_hbm, dvb, 8)
    fetch("dd", dd_hbm, ddb, 9)
    fetch("si", si_hbm, si, 10)

    barrier = pltpu.get_barrier_semaphore()
    partners = [{"seq_2": 1 - ci}]
    partners += [{"seq_1": lax.rem(xi + i, X)} for i in range(1, X)]
    partners += [{"seq_0": lax.rem(zi + i, Z)} for i in range(1, Z)]
    for partner in partners:
        pl.semaphore_signal(barrier, inc=1, device_id=partner, device_id_type=MESH)

    at = lax.broadcasted_iota(jnp.int32, (DH, DH), 0)
    feature = lax.broadcasted_iota(jnp.int32, (DH, DH), 1)
    r_at = at & (R - 1)
    z_at = (at // R) & (Z - 1)
    x_at = (at // (R * Z)) & (X - 1)
    c_at = at // (R * Z * X)
    owner_feature = ((z_at * X + x_at) * C + c_at) * R + r_at
    perm_s[...] = jnp.where(owner_feature == feature, 1.0, 0.0).astype(BF16)

    upper = jnp.where(at <= feature, 1.0, 0.0).astype(BF16)
    copies["ld"].wait()
    quarters = jnp.concatenate([ldb[:, i * DH : (i + 1) * DH] for i in range(4)], axis=0)
    p1, rest = quarters.astype(BF16), None
    rest = quarters - p1.astype(F32)
    p2 = rest.astype(BF16)
    p3 = (rest - p2.astype(F32)).astype(BF16)
    part = dot(p1, upper) + dot(p2, upper) + dot(p3, upper)
    before = jnp.zeros((HEADS, 1), F32)
    for i in range(4):
        piece = part[i * HEADS : (i + 1) * HEADS]
        cum_s[:, i * DH : (i + 1) * DH] = piece + before
        before = before + piece[:, DH - 1 : DH]
    w_s[...] = jnp.exp(before - cum_s[...])
    decay = jnp.broadcast_to(jnp.exp(before), (HEADS, DH))
    for g in range(2):
        for c in range(C):
            for i in range(2):
                bbuf[g, c, DECAY + 4 * i : DECAY + 4 * i + 4, :] = decay[4 * g : 4 * g + 4]

    def spread(src, dst, start):
        @pl.loop(0, 4)
        def _(i):
            rows = src[pl.ds(start + i * 64, 64)].astype(F32)
            dst[pl.ds((start + i * 64) * HEADS, 64 * HEADS), :] = rows.reshape(64 * HEADS, DH)

    for i in range(2):
        copies[f"k{i}"].wait()
        spread(kb, kf, i * half)
    for i in range(2):
        copies[f"v{i}"].wait()
        spread(vb, vf, i * half)
    copies["dq"].wait()
    dqf[...] = dqb[...].astype(F32).reshape(DECODE * HEADS, DH)

    pending = []

    def send(src, dst, send_sem, recv_sem, where):
        copy = pltpu.make_async_remote_copy(
            src_ref=src, dst_ref=dst, send_sem=send_sem, recv_sem=recv_sem,
            device_id=where, device_id_type=MESH,
        )
        copy.start()
        pending.append(copy)
        return copy

    perm = perm_s[...]
    no_rows = jnp.zeros((8, DH), F32)
    core_copy, x_copy, z_copy, zr_copy, xr_copy, cr_copy = ({} for _ in range(6))
    for g in range(2):
        for j in range(4):
            h = 4 * g + j
            k_h = kf[pl.ds(h, GROUP, stride=HEADS), :].astype(BF16)
            v_h = vf[pl.ds(h, GROUP, stride=HEADS), :].astype(BF16)
            vh[h] = v_h
            dq_h = dqf[pl.ds(h, DECODE, stride=HEADS), :]
            left = jnp.concatenate([perm, jnp.concatenate([dq_h, no_rows], axis=0).astype(BF16)], axis=0)
            k_t = dot_nt(left, k_h)
            kT[h] = k_t[:DH].astype(BF16)
            high, low = halves(k_t * w_s[h : h + 1, :])
            state = dot(high, v_h) + dot(low, v_h)
            for c in range(C):
                bbuf.at[g, c][pl.ds(j, DH // 2, stride=4), :] = state[c * 64 : c * 64 + 64]
            bbuf.at[1, g][pl.ds(EXTRA + j, DECODE, stride=4), :] = state[DH : DH + DECODE]
        if g == 0:
            pl.semaphore_wait(barrier, len(partners))
        rows = pl.ds(0, CORE_ROWS if g else EXTRA)
        core_copy[g] = send(
            bbuf.at[g, 1 - ci, rows], cbuf.at[g, rows], core_s.at[g], core_r.at[g], {"seq_2": 1 - ci}
        )

    def core_weights(g):
        own, other = bbuf[g, ci, DECAY : DECAY + 8, :], cbuf[g, DECAY : DECAY + 8, :]
        return jnp.where(first, other, 1.0), jnp.where(first, 1.0, own), own * other

    for g in range(2):
        core_copy[g].wait_recv()
        w_own, w_other, both = core_weights(g)
        for i in range(X):
            rows = slice(i * QUARTER, (i + 1) * QUARTER)
            tbuf[g, i, 0:QUARTER, :] = scaled(w_own, bbuf[g, ci, rows, :]) + scaled(w_other, cbuf[g, rows, :])
            tbuf[g, i, QUARTER : QUARTER + 8, :] = both
        if g:
            w_own, w_other, _ = core_weights(ci)
            for i in range(X):
                rows = slice(EXTRA + 8 * i, EXTRA + 8 * i + 8)
                tbuf[g, i, QUARTER + 8 : X_ROWS, :] = w_own * bbuf[g, ci, rows, :] + w_other * cbuf[g, rows, :]
        rows = pl.ds(0, X_ROWS if g else QUARTER + 8)
        for i in range(1, X):
            there = lax.rem(xi + i, X)
            x_copy[g, i] = send(
                tbuf.at[g, there, rows], xbuf.at[g, xi, rows], x_s.at[g, i], x_r.at[g, i], {"seq_1": there}
            )
        xbuf[g, xi, rows, :] = tbuf[g, xi, rows, :]

    causal = lax.broadcasted_iota(jnp.int32, (DH, DH), 0) >= lax.broadcasted_iota(jnp.int32, (DH, DH), 1)

    def block_attention(start, stop):
        @pl.loop(start, stop)
        def _(h):
            q_h = qf[pl.ds(h, GROUP, stride=HEADS), :].astype(BF16)
            qp[h] = dot_nt(q_h, perm_s[...]).astype(BF16)
            row = cum_s[pl.ds(h, 1), :]
            column = jnp.broadcast_to(row, (DH, GROUP)).T
            ecol[h] = jnp.exp(column)
            for i in range(4):
                span = (i + 1) * DH
                scores = dot(qp[h, i * DH : span, :], kT[h, :, 0:span])
                here = column[i * DH : span]
                parts = []
                for j in range(i + 1):
                    cut = slice(j * DH, (j + 1) * DH)
                    gap = here - row[:, cut]
                    if j == i:
                        gap = jnp.where(causal, gap, -jnp.inf)
                    parts.append((scores[:, cut] * jnp.exp(gap)).astype(BF16))
                masked = jnp.concatenate(parts, axis=1) if i else parts[0]
                intra[h, i * DH : span, :] = dot(masked, vh[h, 0:span, :])

    copies["q"].wait()
    spread(qb, qf, 0)
    spread(qb, qf, half)
    block_attention(*FILL[0])

    for g in range(2):
        for i in range(1, X):
            x_copy[g, i].wait_recv()

        def row_total(g, part, tile):
            total, length = None, None
            for i in range(X):
                step = xbuf[tile, i, QUARTER : QUARTER + 8, :]
                rows = xbuf[g, i, part, :]
                total = rows if total is None else scaled(step, total) + rows
                length = step if length is None else length * step
            return total, length

        total, length = row_total(g, slice(0, QUARTER), g)
        for i in range(Z):
            rbuf[g, i, 0:ZR, :] = total[i * ZR : (i + 1) * ZR]
            rbuf[g, i, ZR : ZR + 8, :] = length
        if g:
            total, _ = row_total(g, slice(QUARTER + 8, X_ROWS), ci)
            for i in range(Z):
                rbuf[g, i, ZR + 8 : ZR + 16, :] = total
        rows = pl.ds(0, ZR + 16 if g else ZR + 8)
        for i in range(1, Z):
            there = lax.rem(zi + i, Z)
            z_copy[g, i] = send(
                rbuf.at[g, there, rows], zbuf.at[g, zi, rows], z_s.at[g, i], z_r.at[g, i], {"seq_0": there}
            )
        zbuf[g, zi, rows, :] = rbuf[g, zi, rows, :]

    for name in ("dk", "dv", "dd", "si"):
        copies[name].wait()
    dkf[...] = dkb[...].astype(F32).reshape(DECODE * HEADS, DH)
    dvf[...] = dvb[...].astype(F32).reshape(DECODE * HEADS, DH)
    steps = lax.broadcasted_iota(jnp.int32, (DECODE, HEADS), 0)
    lanes = lax.broadcasted_iota(jnp.int32, (DECODE, HEADS), 1)
    run = jnp.zeros((DECODE, HEADS), F32)
    for u in range(DECODE):
        run = run + jnp.where(steps >= u, ddb[u : u + 1, :], 0.0)
    step_of = lax.broadcasted_iota(jnp.int32, (DECODE, 1), 0)
    for j in range(4):
        h = ci * 4 + j
        run_h = jnp.sum(jnp.where(lanes == h, run, 0.0), axis=1, keepdims=True)
        dq_h = dqf[pl.ds(h, DECODE, stride=HEADS), :]
        dk_h = dkf[pl.ds(h, DECODE, stride=HEADS), :]
        dv_h = dvf[pl.ds(h, DECODE, stride=HEADS), :]
        total = jnp.zeros((DECODE, DH), F32)
        for s in range(DECODE):
            score = jnp.sum(dq_h * dk_h[s : s + 1, :], axis=1, keepdims=True)
            gap = jnp.where(step_of >= s, run_h - run_h[s : s + 1, :], -jnp.inf)
            total = total + (score * jnp.exp(gap)) * dv_h[s : s + 1, :]
        dint[pl.ds(j, DECODE, stride=4), :] = total
        dexp[pl.ds(j, DECODE, stride=4), :] = jnp.broadcast_to(jnp.exp(run_h), (DECODE, DH))
        high, low = halves(si[pl.ds(h, DH, stride=HEADS), :])
        left = jnp.concatenate([dq_h, no_rows], axis=0).astype(BF16)
        rin[pl.ds(j, DECODE, stride=4), :] = (dot(left, high) + dot(left, low))[:DECODE]
    index = (zi * X + xi) * C + ci
    prior = si[pl.ds(pl.multiple_of(index * R * HEADS, 8), R * HEADS), :]
    for g in range(2):
        for r in range(R):
            sitile[g, 4 * r : 4 * r + 4, :] = prior[r * HEADS + 4 * g : r * HEADS + 4 * g + 4]

    block_attention(*FILL[1])

    for g in range(2):
        for i in range(1, Z):
            z_copy[g, i].wait_recv()
        state = sitile[g]
        for i in range(Z):
            zs[g, i] = state
            state = scaled(zbuf[g, i, ZR : ZR + 8, :], state) + zbuf[g, i, 0:ZR, :]
        for i in range(1, Z):
            there = lax.rem(zi + i, Z)
            zr_copy[g, i] = send(zs.at[g, there], zr.at[g, zi], zr_s.at[g, i], zr_r.at[g, i], {"seq_0": there})
        zr[g, zi] = zs[g, zi]
        for r in range(R):
            fs_ref[r, 4 * g : 4 * g + 4, :] = state[4 * r : 4 * r + 4]

    mine = pl.ds(pl.multiple_of(xi * 8, 8), 8)
    reading = rin[mine, :]
    for i in range(Z):
        reading = zbuf[ci, i, ZR : ZR + 8, :] * reading + zbuf[1, i, ZR + 8 : ZR + 16, :]
    reading = dexp[mine, :] * reading + dint[mine, :]
    reading = reading * lax.rsqrt(jnp.mean(reading * reading, axis=-1, keepdims=True) + norm_eps)
    for i in range(X):
        xs[1, i, QUARTER : QUARTER + 8, :] = reading

    block_attention(*FILL[2])

    for g in range(2):
        for i in range(1, Z):
            zr_copy[g, i].wait_recv()
        state = zr[g].reshape(QUARTER, DH)
        for i in range(X):
            xs[g, i, 0:QUARTER, :] = state
            if i < X - 1:
                state = scaled(xbuf[g, i, QUARTER : QUARTER + 8, :], state) + xbuf[g, i, 0:QUARTER, :]
        rows = pl.ds(0, QUARTER + 8 if g else QUARTER)
        for i in range(1, X):
            there = lax.rem(xi + i, X)
            xr_copy[g, i] = send(
                xs.at[g, there, rows], pc.at[g, xi, rows], xr_s.at[g, i], xr_r.at[g, i], {"seq_1": there}
            )
        pc[g, xi, rows, :] = xs[g, xi, rows, :]

    for g in range(2):
        for i in range(1, X):
            xr_copy[g, i].wait_recv()
        zero_decay = jnp.where(first, bbuf[g, ci, DECAY : DECAY + 8, :], cbuf[g, DECAY : DECAY + 8, :])
        for i in range(X):
            rows = slice(i * QUARTER, (i + 1) * QUARTER)
            chip = pc[g, i, 0:QUARTER, :]
            zero = jnp.where(first, bbuf[g, ci, rows, :], cbuf[g, rows, :])
            second = scaled(zero_decay, chip) + zero
            ps[g, rows, :] = jnp.where(first, second, chip)
            pp[g, ci, rows, :] = jnp.where(first, chip, second)
            if g:
                rows = slice(HALF + 8 * i, HALF + 8 * i + 8)
                ps[g, rows, :] = pc[g, i, QUARTER : QUARTER + 8, :]
                pp[g, ci, rows, :] = pc[g, i, QUARTER : QUARTER + 8, :]
        rows = pl.ds(0, HALF + 32 if g else HALF)
        cr_copy[g] = send(ps.at[g, rows], pp.at[g, ci, rows], cr_s.at[g], cr_r.at[g], {"seq_2": 1 - ci})

    outs = []
    for g in range(2):
        cr_copy[g].wait_recv()
        for j in range(4):
            h = 4 * g + j
            state = jnp.concatenate([pp.at[g, c][pl.ds(j, DH // 2, stride=4), :] for c in range(C)], axis=0)
            high, low = halves(state)
            for i in range(2):
                rows = slice(i * half, (i + 1) * half)
                queries = qp[h, rows, :]
                inter = dot(queries, high) + dot(queries, low)
                mixed = intra[h, rows, :] + ecol[h, rows, :] * inter
                mixed = mixed * lax.rsqrt(jnp.mean(mixed * mixed, axis=-1, keepdims=True) + norm_eps)
                ob[h, rows, :] = mixed.astype(BF16)
            outs.append(pltpu.make_async_copy(ob.at[h], out_hbm.at[h], out_sem.at[h]))
            outs[-1].start()
    for c in range(C):
        for i in range(X):
            for t in range(2):
                start = HALF + 8 * i + 4 * t
                dec_ref[2 * i + t, 4 * c : 4 * c + 4, :] = pp[1, c, start : start + 4, :]
    for copy in pending:
        copy.wait_send()
    for copy in outs:
        copy.wait()


def local(Z, q, k, v, log_decay, state_in, dq, dk, dv, dd):
    ZR = QUARTER // Z
    any_ref = pl.BlockSpec(memory_space=pl.ANY)
    vmem = pl.BlockSpec(memory_space=pltpu.VMEM)
    rows = (GROUP, HEADS, DH)
    flat = (GROUP * HEADS, DH)
    few = (DECODE, HEADS, DH)
    per_head = (HEADS, GROUP, DH)
    V, D = pltpu.VMEM, pltpu.SemaphoreType.DMA
    attended, final_rows, decode_out = pl.pallas_call(
        functools.partial(kernel, Z),
        name="scan_attention",
        out_shape=(
            jax.ShapeDtypeStruct(per_head, BF16),
            jax.ShapeDtypeStruct((ZR // 4, HEADS, DH), F32),
            jax.ShapeDtypeStruct(few, F32),
        ),
        in_specs=[any_ref] * 9,
        out_specs=(any_ref, vmem, vmem),
        scratch_shapes=[
            V(rows, BF16), V(rows, BF16), V(rows, BF16),
            V(flat, F32), V(flat, F32), V(flat, F32),
            V((HEADS, GROUP), F32), V((DH * HEADS, DH), F32),
            V(few, BF16), V(few, BF16), V(few, BF16), V((DECODE, HEADS), F32),
            V((DECODE * HEADS, DH), F32), V((DECODE * HEADS, DH), F32), V((DECODE * HEADS, DH), F32),
            V((DH, DH), BF16), V((HEADS, GROUP), F32), V((HEADS, GROUP), F32),
            V((HEADS, DH, GROUP), BF16), V(per_head, BF16), V(per_head, BF16),
            V(per_head, F32), V(per_head, F32), V(per_head, BF16),
            V((2, C, CORE_ROWS, DH), F32), V((2, CORE_ROWS, DH), F32),
            V((2, X, X_ROWS, DH), F32), V((2, X, X_ROWS, DH), F32),
            V((2, Z, ZR + 16, DH), F32), V((2, Z, ZR + 16, DH), F32),
            V((2, Z, ZR, DH), F32), V((2, Z, ZR, DH), F32),
            V((2, X, QUARTER + 8, DH), F32), V((2, X, QUARTER + 8, DH), F32),
            V((2, HALF + 32, DH), F32), V((2, C, HALF + 32, DH), F32),
            V((2, ZR, DH), F32), V((32, DH), F32), V((32, DH), F32), V((32, DH), F32),
            D((11,)), D((HEADS,)),
            D((2,)), D((2,)), D((2, X)), D((2, X)), D((2, Z)), D((2, Z)),
            D((2, Z)), D((2, Z)), D((2, X)), D((2, X)), D((2,)), D((2,)),
        ],
        compiler_params=pltpu.CompilerParams(collective_id=0, has_side_effects=True),
    )(q, k, v, log_decay.T, state_in.reshape(DH * HEADS, DH), dq, dk, dv, dd)
    return jnp.transpose(attended, (1, 0, 2)), final_rows, decode_out


def solution(mesh):
    heads = mesh.shape["head"]
    z = mesh.shape["seq"] // (X * C)
    split = Mesh(mesh.devices.reshape(z, X, C, heads), (*SEQ, "head"))
    return jax.shard_map(
        functools.partial(local, z),
        mesh=split,
        in_specs=(
            P(SEQ, "head", None),
            P(SEQ, "head", None),
            P(SEQ, "head", None),
            P(SEQ, "head"),
            P(None, "head", None),
            P(None, "head", None),
            P(None, "head", None),
            P(None, "head", None),
            P(None, "head"),
        ),
        out_specs=(P(SEQ, "head", None), P(SEQ, "head", None), P(None, "head", None)),
        check_vma=False,
    )
```

time: 134 us -> 42.8 us (0.32)
  blocking collectives: 56.5 us -> 0 us
  Pallas kernels: 0 us -> 37.9 us
  starting transfers between devices: 30.8 us -> 0 us
  waiting for transfers between devices: 15 us -> 0 us
  matrix products: 13.8 us -> 0 us
  other arithmetic: 8.84 us -> 0 us
  local copies, waits for them, and re-layouts: 7.65 us -> 4.11 us
    psum x3 -> x0, blocking collectives: 56.5 us -> none  [one_axis_at_a_time(): return functools.reduce(lax.psum, axes, array)]
    pallas_call x0 -> x1, Pallas kernels: none -> 37.9 us  [local(): pl.pallas_call(functools.partial(kernel, Z), name='scan_attention', out_s...]
    all_to_all x3 -> x0, starting transfers between devices: 30.8 us -> none  [the longest x1 14.8 us: sent_to_all(): return lax.all_to_all(copies, axis, split_axis=0, concat_axis=0, tiled=True)]
    all_to_all x3 -> x0, waiting for transfers between devices: 15 us -> none  [the longest x1 15 us: local(): lax.all_to_all(shard_state[None], SEQ, split_axis=1, concat_axis=0, tiled...]
    dot_general x13 -> x0, matrix products: 13.8 us -> none  [the longest x1 6.14 us: local(): jnp.einsum('nhij,njhd->nihd', masked, values_blk, preferred_element_type=...]
    mul x5 -> x0, other arithmetic: 3.49 us -> none  [the longest x2 1.9 us: local(): key_rows.reshape(blocks, GROUP, heads_here, width).astype(jnp.float32)]
    unnamed x18 -> x7, local copies, waits for them, and re-layouts: 1.53 us -> 4.11 us
    another operation x4 -> x0, other arithmetic: 2.5 us -> none
  transfers between devices with their start and end apart: 3 -> 0, of which waited for: 1 -> 0; matrix products, arithmetic and copies ran while one was open for 13% -> 0% of each run, Pallas kernels for 0% -> 0%
where the time goes in v1:
time: 42.8 us; the launch traced here: 42.7 us
  Pallas kernels  37.9 us (89%)
  local copies, waits for them, and re-layouts  4.11 us (10%)
  between operations  0.66 us (2%)
    pallas_call x1, Pallas kernels, local(): pl.pallas_call(functools.partial(kernel, Z), name='scan_attention', out_s...  37.9 us
    unnamed x7, local copies, waits for them, and re-layouts  4.11 us

profile of v1, /device:TPU:1, one launch (start us, length us, event | category | flops | bytes accessed | tf_op | source)
XLA Modules:
  0.0 42.7 jit_solution(7506436879739701208)
XLA Ops:
  0.6 37.9 %scan_attention.1 = (bf16[8,512,128]{2,1,0:T(8,128)(2,1)}, f32[2,8,128]{2,1,0:T(8,128)}, f32[8,8,128]{2,1,0:T(8,128)}) custom-call(bf16[512,8,128]{2,1,0:T(8,128)(2,1)} %q_hbm.1, bf16[512,8,128]{2,1,0:T(8,128)(2,1)} %k_hbm.1, bf16[512,8,128]{2,1,0:T(8,128)(2,1)} %v_hbm.1, f32[8,512]{1,0:T(8,128)} %bitcast.5, f32[1024,128]{1,0:T(8,128)} %bitcast.4, ...), custom_call_target="tpu_custom_call" | custom-call | tf_op jit(solution)/shard_map/scan_attention/pallas_call | solution.py:384
  38.6 0.0 copy-start.1
  38.6 0.0 copy-start
  38.6 2.9 %copy.12 = bf16[512,8,128]{2,1,0:T(8,128)(2,1)} copy(bf16[512,8,128]{2,0,1:T(8,128)(2,1)} %bitcast.3) | data formatting | bytes 2097152
  41.5 0.0 copy-done.1
  41.5 0.6 %copy.15 = f32[2,8,128]{2,1,0:T(8,128)} copy(f32[2,8,128]{2,1,0:T(8,128)S(1)} %copy-done.1) | data formatting | bytes 16384
  42.1 0.0 copy-done
  42.1 0.6 %copy.16 = f32[8,8,128]{2,1,0:T(8,128)} copy(f32[8,8,128]{2,1,0:T(8,128)S(1)} %copy-done) | data formatting | bytes 65536
Async XLA Ops:
  38.6 2.9 %copy-start.1 = (f32[2,8,128]{2,1,0:T(8,128)S(1)}, f32[2,8,128]{2,1,0:T(8,128)}, u32[]{:S(2)}) copy-start(f32[2,8,128]{2,1,0:T(8,128)} %get-tuple-element.16) | copy-start | bytes 24580
  38.6 3.5 %copy-start = (f32[8,8,128]{2,1,0:T(8,128)S(1)}, f32[8,8,128]{2,1,0:T(8,128)}, u32[]{:S(2)}) copy-start(f32[8,8,128]{2,1,0:T(8,128)} %get-tuple-element.17) | copy-start | bytes 98308

commit v2 on v1

--- a/solution.py
+++ b/solution.py
@@ -49,18 +49,23 @@
 def kernel(
     Z,
     q_hbm, k_hbm, v_hbm, ld_hbm, si_hbm, dq_hbm, dk_hbm, dv_hbm, dd_hbm,
-    out_hbm, fs_ref, dec_ref,
+    intra, ecol, qp, pp, fs_ref, dall,
     kb, vb, qb, kf, vf, qf, ldb, si, dqb, dkb, dvb, ddb, dqf, dkf, dvf,
-    perm_s, cum_s, w_s, kT, vh, qp, ecol, intra, ob,
-    bbuf, cbuf, tbuf, xbuf, rbuf, zbuf, zs, zr, xs, pc, ps, pp,
-    sitile, rin, dint, dexp,
-    in_sem, out_sem,
-    core_s, core_r, x_s, x_r, z_s, z_r, zr_s, zr_r, xr_s, xr_r, cr_s, cr_r,
+    perm_s, cum_s, w_s, kT, vh,
+    bbuf, cbuf, tbuf, xbuf, rbuf, zbuf, zs, zr, xs, pc, ps,
+    sitile, base, after, rin, dint, dexp, dread, dx,
+    ready, in_sem,
+    core_s, core_r, x_s, x_r, z_s, z_r, zr_s, zr_r, xr_s, xr_r, cr_s, cr_r, d_s, d_r, dc_s, dc_r,
 ):
     ZR = QUARTER // Z
     R = ZR // 4
+    ZH = Z // 2
+    PAIR = 2 * ZR
     zi, xi, ci = (lax.axis_index(a) for a in SEQ)
     first = ci == 0
+    place = lax.rem(zi, ZH)
+    line = zi - place
+    upper_half = zi >= ZH
 
     half = GROUP // 2
     copies = {}
@@ -86,14 +91,18 @@
     barrier = pltpu.get_barrier_semaphore()
     partners = [{"seq_2": 1 - ci}]
     partners += [{"seq_1": lax.rem(xi + i, X)} for i in range(1, X)]
-    partners += [{"seq_0": lax.rem(zi + i, Z)} for i in range(1, Z)]
     for partner in partners:
         pl.semaphore_signal(barrier, inc=1, device_id=partner, device_id_type=MESH)
+    for i in range(1, Z):
+
+        @pl.when(zi + i < Z)
+        def _():
+            pl.semaphore_signal(barrier, inc=1, device_id={"seq_0": zi + i}, device_id_type=MESH)
 
     at = lax.broadcasted_iota(jnp.int32, (DH, DH), 0)
     feature = lax.broadcasted_iota(jnp.int32, (DH, DH), 1)
     r_at = at & (R - 1)
-    z_at = (at // R) & (Z - 1)
+    z_at = ((at // R) & 1) * ZH + ((at // (2 * R)) & (ZH - 1))
     x_at = (at // (R * Z)) & (X - 1)
     c_at = at // (R * Z * X)
     owner_feature = ((z_at * X + x_at) * C + c_at) * R + r_at
@@ -119,6 +128,13 @@
             for i in range(2):
                 bbuf[g, c, DECAY + 4 * i : DECAY + 4 * i + 4, :] = decay[4 * g : 4 * g + 4]
 
+    pl.semaphore_wait(barrier, len(partners) + zi)
+    for i in range(1, Z):
+
+        @pl.when(zi >= i)
+        def _():
+            pl.semaphore_signal(ready.at[zi], inc=1, device_id={"seq_0": zi - i}, device_id_type=MESH)
+
     def spread(src, dst, start):
         @pl.loop(0, 4)
         def _(i):
@@ -163,8 +179,6 @@
             for c in range(C):
                 bbuf.at[g, c][pl.ds(j, DH // 2, stride=4), :] = state[c * 64 : c * 64 + 64]
             bbuf.at[1, g][pl.ds(EXTRA + j, DECODE, stride=4), :] = state[DH : DH + DECODE]
-        if g == 0:
-            pl.semaphore_wait(barrier, len(partners))
         rows = pl.ds(0, CORE_ROWS if g else EXTRA)
         core_copy[g] = send(
             bbuf.at[g, 1 - ci, rows], cbuf.at[g, rows], core_s.at[g], core_r.at[g], {"seq_2": 1 - ci}
@@ -223,6 +237,21 @@
     spread(qb, qf, half)
     block_attention(*FILL[0])
 
+    def z_rows(g):
+        return pl.ds(0, PAIR + 16 if g else PAIR + 8)
+
+    def send_total(g, slot, there, meet):
+        if meet:
+
+            @pl.when(there > zi)
+            def _():
+                pl.semaphore_wait(ready.at[there], 1)
+
+        return send(
+            rbuf.at[g, lax.rem(there, ZH), z_rows(g)], zbuf.at[g, zi, z_rows(g)],
+            z_s.at[g, slot], z_r.at[g, slot], {"seq_0": there},
+        )
+
     for g in range(2):
         for i in range(1, X):
             x_copy[g, i].wait_recv()
@@ -237,20 +266,19 @@
             return total, length
 
         total, length = row_total(g, slice(0, QUARTER), g)
-        for i in range(Z):
-            rbuf[g, i, 0:ZR, :] = total[i * ZR : (i + 1) * ZR]
-            rbuf[g, i, ZR : ZR + 8, :] = length
+        for i in range(ZH):
+            rbuf[g, i, 0:PAIR, :] = total[i * PAIR : (i + 1) * PAIR]
+            rbuf[g, i, PAIR : PAIR + 8, :] = length
         if g:
             total, _ = row_total(g, slice(QUARTER + 8, X_ROWS), ci)
-            for i in range(Z):
-                rbuf[g, i, ZR + 8 : ZR + 16, :] = total
-        rows = pl.ds(0, ZR + 16 if g else ZR + 8)
-        for i in range(1, Z):
-            there = lax.rem(zi + i, Z)
-            z_copy[g, i] = send(
-                rbuf.at[g, there, rows], zbuf.at[g, zi, rows], z_s.at[g, i], z_r.at[g, i], {"seq_0": there}
-            )
-        zbuf[g, zi, rows, :] = rbuf[g, zi, rows, :]
+            for i in range(ZH):
+                rbuf[g, i, PAIR + 8 : PAIR + 16, :] = total
+        zbuf[g, zi, z_rows(g), :] = rbuf[g, place, z_rows(g), :]
+        for i in range(1, ZH):
+            z_copy[g, i] = send_total(g, i, line + lax.rem(place + i, ZH), g == 0)
+    for g in range(2):
+        for i in range(ZH):
+            z_copy[g, ZH + i] = send_total(g, ZH + i, ZH - line + lax.rem(place + i, ZH), g == 0)
 
     for name in ("dk", "dv", "dd", "si"):
         copies[name].wait()
@@ -278,54 +306,89 @@
         high, low = halves(si[pl.ds(h, DH, stride=HEADS), :])
         left = jnp.concatenate([dq_h, no_rows], axis=0).astype(BF16)
         rin[pl.ds(j, DECODE, stride=4), :] = (dot(left, high) + dot(left, low))[:DECODE]
-    index = (zi * X + xi) * C + ci
-    prior = si[pl.ds(pl.multiple_of(index * R * HEADS, 8), R * HEADS), :]
-    for g in range(2):
-        for r in range(R):
-            sitile[g, 4 * r : 4 * r + 4, :] = prior[r * HEADS + 4 * g : r * HEADS + 4 * g + 4]
+    for t in range(2):
+        index = ((place + t * ZH) * X + xi) * C + ci
+        prior = si[pl.ds(pl.multiple_of(index * R * HEADS, 8), R * HEADS), :]
+        for g in range(2):
+            for r in range(R):
+                start = t * ZR + 4 * r
+                sitile[g, start : start + 4, :] = prior[r * HEADS + 4 * g : r * HEADS + 4 * g + 4]
 
     block_attention(*FILL[1])
 
-    for g in range(2):
-        for i in range(1, Z):
+    def passed(g, state, z):
+        return scaled(zbuf[g, z, PAIR : PAIR + 8, :], state) + zbuf[g, z, 0:PAIR, :]
+
+    for g in range(2):
+        for i in range(1, ZH):
             z_copy[g, i].wait_recv()
-        state = sitile[g]
-        for i in range(Z):
+
+        @pl.when(upper_half)
+        def _():
+            for i in range(ZH):
+                z_copy[g, ZH + i].wait_recv()
+            state = sitile[g]
+            for i in range(ZH):
+                state = passed(g, state, i)
+            base[g] = state
+
+        @pl.when(jnp.logical_not(upper_half))
+        def _():
+            base[g] = sitile[g]
+
+        state = base[g]
+        for i in range(ZH):
             zs[g, i] = state
-            state = scaled(zbuf[g, i, ZR : ZR + 8, :], state) + zbuf[g, i, 0:ZR, :]
-        for i in range(1, Z):
-            there = lax.rem(zi + i, Z)
-            zr_copy[g, i] = send(zs.at[g, there], zr.at[g, zi], zr_s.at[g, i], zr_r.at[g, i], {"seq_0": there})
-        zr[g, zi] = zs[g, zi]
+            state = passed(g, state, line + i)
+        after[g] = state
+        zr[g, place] = zs[g, place]
+        for i in range(1, ZH):
+            there = lax.rem(place + i, ZH)
+            zr_copy[g, i] = send(
+                zs.at[g, there], zr.at[g, place], zr_s.at[g, i], zr_r.at[g, i], {"seq_0": line + there}
+            )
+
+    block_attention(*FILL[2])
+
+    for g in range(2):
+        for i in range(1, ZH):
+            zr_copy[g, i].wait_recv()
+        state = zr[g].reshape(QUARTER, DH)
+        for i in range(X):
+            xs[g, i] = state
+            if i < X - 1:
+                state = scaled(xbuf[g, i, QUARTER : QUARTER + 8, :], state) + xbuf[g, i, 0:QUARTER, :]
+        for i in range(1, X):
+            there = lax.rem(xi + i, X)
+            xr_copy[g, i] = send(xs.at[g, there], pc.at[g, xi], xr_s.at[g, i], xr_r.at[g, i], {"seq_1": there})
+        pc[g, xi] = xs[g, xi]
+
+    @pl.when(jnp.logical_not(upper_half))
+    def _():
+        for g in range(2):
+            for i in range(ZH):
+                z_copy[g, ZH + i].wait_recv()
+            state = after[g]
+            for i in range(ZH, Z):
+                state = passed(g, state, i)
+            after[g] = state
+
+    for g in range(2):
+        state = after[g, pl.ds(pl.multiple_of((zi // ZH) * ZR, 8), ZR), :]
         for r in range(R):
             fs_ref[r, 4 * g : 4 * g + 4, :] = state[4 * r : 4 * r + 4]
-
     mine = pl.ds(pl.multiple_of(xi * 8, 8), 8)
     reading = rin[mine, :]
     for i in range(Z):
-        reading = zbuf[ci, i, ZR : ZR + 8, :] * reading + zbuf[1, i, ZR + 8 : ZR + 16, :]
+        reading = zbuf[ci, i, PAIR : PAIR + 8, :] * reading + zbuf[1, i, PAIR + 8 : PAIR + 16, :]
     reading = dexp[mine, :] * reading + dint[mine, :]
     reading = reading * lax.rsqrt(jnp.mean(reading * reading, axis=-1, keepdims=True) + norm_eps)
-    for i in range(X):
-        xs[1, i, QUARTER : QUARTER + 8, :] = reading
-
-    block_attention(*FILL[2])
-
-    for g in range(2):
-        for i in range(1, Z):
-            zr_copy[g, i].wait_recv()
-        state = zr[g].reshape(QUARTER, DH)
-        for i in range(X):
-            xs[g, i, 0:QUARTER, :] = state
-            if i < X - 1:
-                state = scaled(xbuf[g, i, QUARTER : QUARTER + 8, :], state) + xbuf[g, i, 0:QUARTER, :]
-        rows = pl.ds(0, QUARTER + 8 if g else QUARTER)
-        for i in range(1, X):
-            there = lax.rem(xi + i, X)
-            xr_copy[g, i] = send(
-                xs.at[g, there, rows], pc.at[g, xi, rows], xr_s.at[g, i], xr_r.at[g, i], {"seq_1": there}
-            )
-        pc[g, xi, rows, :] = xs[g, xi, rows, :]
+    dread[...] = reading
+    dx[xi] = reading
+    d_copy = [None]
+    for i in range(1, X):
+        there = lax.rem(xi + i, X)
+        d_copy.append(send(dread, dx.at[xi], d_s.at[i], d_r.at[i], {"seq_1": there}))
 
     for g in range(2):
         for i in range(1, X):
@@ -333,47 +396,57 @@
         zero_decay = jnp.where(first, bbuf[g, ci, DECAY : DECAY + 8, :], cbuf[g, DECAY : DECAY + 8, :])
         for i in range(X):
             rows = slice(i * QUARTER, (i + 1) * QUARTER)
-            chip = pc[g, i, 0:QUARTER, :]
+            chip = pc[g, i]
             zero = jnp.where(first, bbuf[g, ci, rows, :], cbuf[g, rows, :])
             second = scaled(zero_decay, chip) + zero
             ps[g, rows, :] = jnp.where(first, second, chip)
             pp[g, ci, rows, :] = jnp.where(first, chip, second)
-            if g:
-                rows = slice(HALF + 8 * i, HALF + 8 * i + 8)
-                ps[g, rows, :] = pc[g, i, QUARTER : QUARTER + 8, :]
-                pp[g, ci, rows, :] = pc[g, i, QUARTER : QUARTER + 8, :]
-        rows = pl.ds(0, HALF + 32 if g else HALF)
-        cr_copy[g] = send(ps.at[g, rows], pp.at[g, ci, rows], cr_s.at[g], cr_r.at[g], {"seq_2": 1 - ci})
-
-    outs = []
+        cr_copy[g] = send(ps.at[g], pp.at[g, ci], cr_s.at[g], cr_r.at[g], {"seq_2": 1 - ci})
+    for i in range(1, X):
+        d_copy[i].wait_recv()
+    dall[ci] = dx[...]
+    dc_copy = send(dx, dall.at[ci], dc_s, dc_r, {"seq_2": 1 - ci})
+
     for g in range(2):
         cr_copy[g].wait_recv()
-        for j in range(4):
-            h = 4 * g + j
-            state = jnp.concatenate([pp.at[g, c][pl.ds(j, DH // 2, stride=4), :] for c in range(C)], axis=0)
-            high, low = halves(state)
-            for i in range(2):
-                rows = slice(i * half, (i + 1) * half)
-                queries = qp[h, rows, :]
-                inter = dot(queries, high) + dot(queries, low)
-                mixed = intra[h, rows, :] + ecol[h, rows, :] * inter
-                mixed = mixed * lax.rsqrt(jnp.mean(mixed * mixed, axis=-1, keepdims=True) + norm_eps)
-                ob[h, rows, :] = mixed.astype(BF16)
-            outs.append(pltpu.make_async_copy(ob.at[h], out_hbm.at[h], out_sem.at[h]))
-            outs[-1].start()
+    dc_copy.wait_recv()
+    for copy in pending:
+        copy.wait_send()
+
+
+def finish(
+    intra, ecol, qp, pp, fs, dall, out_hbm, fs_hbm, dec_hbm, high_s, low_s, flat, ob, dec, sem
+):
+    copies = [pltpu.make_async_copy(fs, fs_hbm, sem.at[0])]
+    copies[-1].start()
     for c in range(C):
         for i in range(X):
             for t in range(2):
-                start = HALF + 8 * i + 4 * t
-                dec_ref[2 * i + t, 4 * c : 4 * c + 4, :] = pp[1, c, start : start + 4, :]
-    for copy in pending:
-        copy.wait_send()
-    for copy in outs:
+                dec[2 * i + t, 4 * c : 4 * c + 4, :] = dall[c, i, 4 * t : 4 * t + 4, :]
+    copies.append(pltpu.make_async_copy(dec, dec_hbm, sem.at[1]))
+    copies[-1].start()
+    for h in range(HEADS):
+        g, j = divmod(h, 4)
+        state = jnp.concatenate([pp.at[g, c][pl.ds(j, DH // 2, stride=4), :] for c in range(C)], axis=0)
+        high_s[h], low_s[h] = halves(state)
+    for i in range(4):
+        rows = slice(i * DH, (i + 1) * DH)
+        for h in range(HEADS):
+            queries = qp[h, rows, :]
+            inter = dot(queries, high_s[h]) + dot(queries, low_s[h])
+            mixed = intra[h, rows, :] + ecol[h, rows, :] * inter
+            mixed = mixed * lax.rsqrt(jnp.mean(mixed * mixed, axis=-1, keepdims=True) + norm_eps)
+            flat[pl.ds(i * DH * HEADS + h, DH, stride=HEADS), :] = mixed
+        ob[rows] = flat[i * DH * HEADS : (i + 1) * DH * HEADS, :].reshape(DH, HEADS, DH).astype(BF16)
+        copies.append(pltpu.make_async_copy(ob.at[rows], out_hbm.at[rows], sem.at[2 + i]))
+        copies[-1].start()
+    for copy in copies:
         copy.wait()
 
 
 def local(Z, q, k, v, log_decay, state_in, dq, dk, dv, dd):
     ZR = QUARTER // Z
+    ZH, PAIR = Z // 2, 2 * ZR
     any_ref = pl.BlockSpec(memory_space=pl.ANY)
     vmem = pl.BlockSpec(memory_space=pltpu.VMEM)
     rows = (GROUP, HEADS, DH)
@@ -381,16 +454,16 @@
     few = (DECODE, HEADS, DH)
     per_head = (HEADS, GROUP, DH)
     V, D = pltpu.VMEM, pltpu.SemaphoreType.DMA
-    attended, final_rows, decode_out = pl.pallas_call(
+    args = (q, k, v, log_decay.T, state_in.reshape(DH * HEADS, DH), dq, dk, dv, dd)
+    parts = pl.pallas_call(
         functools.partial(kernel, Z),
         name="scan_attention",
         out_shape=(
-            jax.ShapeDtypeStruct(per_head, BF16),
-            jax.ShapeDtypeStruct((ZR // 4, HEADS, DH), F32),
-            jax.ShapeDtypeStruct(few, F32),
+            V(per_head, F32), V(per_head, F32), V(per_head, BF16), V((2, C, HALF, DH), F32),
+            V((ZR // 4, HEADS, DH), F32), V((C, X, 8, DH), F32),
         ),
         in_specs=[any_ref] * 9,
-        out_specs=(any_ref, vmem, vmem),
+        out_specs=[vmem] * 6,
         scratch_shapes=[
             V(rows, BF16), V(rows, BF16), V(rows, BF16),
             V(flat, F32), V(flat, F32), V(flat, F32),
@@ -398,22 +471,40 @@
             V(few, BF16), V(few, BF16), V(few, BF16), V((DECODE, HEADS), F32),
             V((DECODE * HEADS, DH), F32), V((DECODE * HEADS, DH), F32), V((DECODE * HEADS, DH), F32),
             V((DH, DH), BF16), V((HEADS, GROUP), F32), V((HEADS, GROUP), F32),
-            V((HEADS, DH, GROUP), BF16), V(per_head, BF16), V(per_head, BF16),
-            V(per_head, F32), V(per_head, F32), V(per_head, BF16),
+            V((HEADS, DH, GROUP), BF16), V(per_head, BF16),
             V((2, C, CORE_ROWS, DH), F32), V((2, CORE_ROWS, DH), F32),
             V((2, X, X_ROWS, DH), F32), V((2, X, X_ROWS, DH), F32),
-            V((2, Z, ZR + 16, DH), F32), V((2, Z, ZR + 16, DH), F32),
-            V((2, Z, ZR, DH), F32), V((2, Z, ZR, DH), F32),
-            V((2, X, QUARTER + 8, DH), F32), V((2, X, QUARTER + 8, DH), F32),
-            V((2, HALF + 32, DH), F32), V((2, C, HALF + 32, DH), F32),
-            V((2, ZR, DH), F32), V((32, DH), F32), V((32, DH), F32), V((32, DH), F32),
-            D((11,)), D((HEADS,)),
+            V((2, ZH, PAIR + 16, DH), F32), V((2, Z, PAIR + 16, DH), F32),
+            V((2, ZH, PAIR, DH), F32), V((2, ZH, PAIR, DH), F32),
+            V((2, X, QUARTER, DH), F32), V((2, X, QUARTER, DH), F32),
+            V((2, HALF, DH), F32),
+            V((2, PAIR, DH), F32), V((2, PAIR, DH), F32), V((2, PAIR, DH), F32),
+            V((32, DH), F32), V((32, DH), F32), V((32, DH), F32),
+            V((8, DH), F32), V((X, 8, DH), F32),
+            pltpu.SemaphoreType.REGULAR((Z,)), D((11,)),
             D((2,)), D((2,)), D((2, X)), D((2, X)), D((2, Z)), D((2, Z)),
-            D((2, Z)), D((2, Z)), D((2, X)), D((2, X)), D((2,)), D((2,)),
+            D((2, ZH)), D((2, ZH)), D((2, X)), D((2, X)), D((2,)), D((2,)),
+            D((X,)), D((X,)), D(()), D(()),
         ],
-        compiler_params=pltpu.CompilerParams(collective_id=0, has_side_effects=True),
-    )(q, k, v, log_decay.T, state_in.reshape(DH * HEADS, DH), dq, dk, dv, dd)
-    return jnp.transpose(attended, (1, 0, 2)), final_rows, decode_out
+        compiler_params=pltpu.CompilerParams(
+            collective_id=0, has_side_effects=True, vmem_limit_bytes=32 << 20
+        ),
+    )(*(pltpu.with_memory_space_constraint(arg, pltpu.HBM) for arg in args))
+    return pl.pallas_call(
+        finish,
+        name="finish",
+        out_shape=(
+            jax.ShapeDtypeStruct(rows, BF16),
+            jax.ShapeDtypeStruct((ZR // 4, HEADS, DH), F32),
+            jax.ShapeDtypeStruct(few, F32),
+        ),
+        in_specs=[vmem] * 6,
+        out_specs=[any_ref] * 3,
+        scratch_shapes=[
+            V((HEADS, DH, DH), BF16), V((HEADS, DH, DH), BF16), V(flat, F32), V(rows, BF16), V(few, F32), D((6,)),
+        ],
+        compiler_params=pltpu.CompilerParams(vmem_limit_bytes=16 << 20),
+    )(*(pltpu.with_memory_space_constraint(part, pltpu.VMEM) for part in parts))
 
 
 def solution(mesh):

time: 42.8 us -> 36.3 us (0.85)
  local copies, waits for them, and re-layouts: 4.11 us -> 0 us
  Pallas kernels: 37.9 us -> 35.4 us
    pallas_call x1, Pallas kernels: 37.9 us -> 33.5 us  [local(): pl.pallas_call(functools.partial(kernel, Z), name='scan_attention', out_s...]
    unnamed x7 -> x0, local copies, waits for them, and re-layouts: 4.11 us -> none
    pallas_call x0 -> x1, Pallas kernels: none -> 1.9 us  [local(): pl.pallas_call(finish, name='finish', out_shape=(jax.ShapeDtypeStruct(row...]
where the time goes in v2:
time: 36.3 us; the launch traced here: 36.1 us
  Pallas kernels  35.4 us (98%)
  between operations  0.64 us (2%)
    pallas_call x1, Pallas kernels, local(): pl.pallas_call(functools.partial(kernel, Z), name='scan_attention', out_s...  33.5 us
    pallas_call x1, Pallas kernels, local(): pl.pallas_call(finish, name='finish', out_shape=(jax.ShapeDtypeStruct(row...  1.9 us

profile of v2, /device:TPU:1, one launch (start us, length us, event | category | flops | bytes accessed | tf_op | source)
XLA Modules:
  0.0 36.1 jit_solution(13386890110750899386)
XLA Ops:
  0.6 33.5 %scan_attention.1 = (f32[8,512,128]{2,1,0:T(8,128)S(1)}, f32[8,512,128]{2,1,0:T(8,128)S(1)}, bf16[8,512,128]{2,1,0:T(8,128)(2,1)S(1)}, f32[2,2,256,128]{3,2,1,0:...) custom-call(bf16[512,8,128]{2,1,0:T(8,128)(2,1)} %q_hbm.1, bf16[512,8,128]{2,1,0:T(8,128)(2,1)} %k_hbm.1, ...), custom_call_target="tpu_custom_call" | custom-call | tf_op jit(solution)/shard_map/scan_attention/pallas_call | solution.py:458
  34.2 1.9 %finish.1 = (bf16[512,8,128]{2,1,0:T(8,128)(2,1)}, f32[2,8,128]{2,1,0:T(8,128)}, f32[8,8,128]{2,1,0:T(8,128)}) custom-call(f32[8,512,128]{2,1,0:T(8,128)S(1)} %get-tuple-element.9.intra, f32[8,512,128]{2,1,0:T(8,128)S(1)} %get-tuple-element.10.ecol, bf16[8,512,128]{2,1,0:T(8,128)(2,1)S(1)} %get-tuple-element.11.qp, ...), custom_call_target="tpu_custom_call" | custom-call | tf_op jit(solution)/shard_map/finish/pallas_call | solution.py:493
